TPU v7x, 32 devices: a whole 2x2x4 slice. The times are simulated.
32 devices in a mesh: dp: 16 (over z, x, core), tensor: 2 (over y).
Axes of the slice: x: 2, y: 2, z: 4, core: 2. Of those that a mesh axis runs over, the one named last changes fastest.
Arguments:
- tokens: bfloat16 [16384, 1536], P(('dp', 'tensor')), may hold values from -6 to 6
- seg_ids: int32 [16384], P('dp'), may hold values from 0 to 4, as said below
- gain_attn: bfloat16 [1536], P('dp'), may hold values from 0.5 to 1.5
- w_query: bfloat16 [1536, 1536], P('dp', 'tensor'), may hold values from -0.21875 to 0.21875
- w_key: bfloat16 [1536, 1536], P('dp', 'tensor'), may hold values from -0.21875 to 0.21875
- w_value: bfloat16 [1536, 1536], P('dp', 'tensor'), may hold values from -0.15625 to 0.15625
- w_outgate: bfloat16 [1536, 1536], P('dp', 'tensor'), may hold values from -0.15625 to 0.15625
- w_forget: bfloat16 [1536, 24], P('dp', 'tensor'), may hold values from -0.15625 to 0.15625
- forget_bias: bfloat16 [24], P('tensor'), may hold values from 1 to 7
- w_out: bfloat16 [1536, 1536], P('dp', 'tensor'), may hold values from -0.875 to 0.875
- gain_mlp: bfloat16 [1536], P('dp'), may hold values from 0.5 to 1.5
- w_gate: bfloat16 [1536, 4096], P('dp', 'tensor'), may hold values from -0.15625 to 0.15625
- w_up: bfloat16 [1536, 4096], P('dp', 'tensor'), may hold values from -0.15625 to 0.15625
- w_down: bfloat16 [1536, 4096], P('dp', 'tensor'), may hold values from -0.09375 to 0.09375
- grad_output: bfloat16 [16384, 1536], P(('dp', 'tensor')), may hold values from -6 to 6
Outputs:
- output: bfloat16 [16384, 1536], P(('dp', 'tensor'))
- grad_tokens: bfloat16 [16384, 1536], P(('dp', 'tensor'))
- grad_gain_attn: float32 [1536], P('dp')
- grad_w_query: float32 [1536, 1536], P('dp', 'tensor')
- grad_w_key: float32 [1536, 1536], P('dp', 'tensor')
- grad_w_value: float32 [1536, 1536], P('dp', 'tensor')
- grad_w_outgate: float32 [1536, 1536], P('dp', 'tensor')
- grad_w_forget: float32 [1536, 24], P('dp', 'tensor')
- grad_forget_bias: float32 [24], P('tensor')
- grad_w_out: float32 [1536, 1536], P('dp', 'tensor')
- grad_gain_mlp: float32 [1536], P('dp')
- grad_w_gate: float32 [1536, 4096], P('dp', 'tensor')
- grad_w_up: float32 [1536, 4096], P('dp', 'tensor')
- grad_w_down: float32 [1536, 4096], P('dp', 'tensor')
Inputs may be any that keep to these rules, and one draw needn't show every extreme that they name: `seg_ids`: each sequence of 1024 rows holds 4 documents numbered 1 to 4 in order, each of one or more tokens, followed by 1 to 128 padding tokens with id 0.
All inputs are finite; a program needn't handle non-finite values.
Results may differ from a plain program's by a relative error of at most 0.015.
Values may be sent and summed in bfloat16 or wider, within the bound.
A program may use at most 320 MiB of HBM per device.

v0:
```python
import jax
import jax.numpy as jnp
from jax import lax
from jax.sharding import PartitionSpec as P

LEN = 1024


epsilon = 1e-06


def to_low(value):
    return value.astype(jnp.bfloat16)


def dot_plain(left, right):
    return jnp.dot(left, right, preferred_element_type=jnp.float32)


def dot_rows(left, right):
    return lax.dot_general(
        left, right, (((1,), (1,)), ((), ())), preferred_element_type=jnp.float32
    )


def dot_cols(left, right):
    return lax.dot_general(
        left, right, (((0,), (0,)), ((), ())), preferred_element_type=jnp.float32
    )


def fold_parts(received, parts):
    return jnp.sum(
        received.reshape((parts, received.shape[0] // parts) + received.shape[1:]), axis=0
    )


def norm_forward(values, gain):
    inverse = lax.rsqrt(jnp.mean(values * values, axis=-1, keepdims=True) + epsilon)
    unit_rows = values * inverse
    return (unit_rows, inverse, unit_rows * gain)


def norm_backward(grad_normed, unit_rows, inverse, gain):
    grad_unit = grad_normed * gain
    centred = grad_unit - unit_rows * jnp.mean(grad_unit * unit_rows, axis=-1, keepdims=True)
    return (inverse * centred, jnp.sum(grad_normed * unit_rows, axis=0))


def block_mask(seg_block, seg_all, row_start, block_size):
    length = seg_all.shape[0]
    query_pos = row_start + lax.broadcasted_iota(jnp.int32, (block_size, length), 0)
    key_pos = lax.broadcasted_iota(jnp.int32, (block_size, length), 1)
    allowed = (
        (seg_block[:, None] == seg_all[None, :]) & (seg_all[None, :] != 0) & (key_pos <= query_pos)
    )
    return allowed | (key_pos == query_pos)


def block_logits(query_block, keys_all, cumul_block, cumul_all, allowed):
    qk_scale = query_block.shape[2] ** (-0.5)
    logits = (
        jnp.einsum("qhd,khd->hqk", query_block, keys_all, preferred_element_type=jnp.float32)
        * qk_scale
    )
    logits = logits + cumul_block.T[:, :, None] - cumul_all.T[:, None, :]
    return jnp.where(allowed[None], logits, -1e30)


def attend_forward(packed):
    queries, keys_all, values_all, cumulative, segments = packed
    length = queries.shape[0]
    block_size = min(512, length)
    outputs = []
    log_sums = []
    for row_start in range(0, length, block_size):
        row_end = row_start + block_size
        allowed = block_mask(segments[row_start:row_end], segments, row_start, block_size)
        logits = block_logits(
            queries[row_start:row_end], keys_all, cumulative[row_start:row_end], cumulative, allowed
        )
        largest = jnp.max(logits, axis=2, keepdims=True)
        exponent = jnp.exp(logits - largest)
        row_total = jnp.sum(exponent, axis=2, keepdims=True)
        attn_probs = to_low(exponent / row_total)
        outputs.append(
            jnp.einsum("hqk,khd->qhd", attn_probs, values_all, preferred_element_type=jnp.float32)
        )
        log_sums.append(largest[:, :, 0] + jnp.log(row_total[:, :, 0]))
    return (jnp.concatenate(outputs, axis=0), jnp.concatenate(log_sums, axis=1))


def attend_backward(packed):
    queries, keys_all, values_all, cumulative, segments, log_sums, grad_attended = packed
    length = queries.shape[0]
    block_size = min(512, length)
    qk_scale = queries.shape[2] ** (-0.5)
    grad_keys = jnp.zeros(keys_all.shape, jnp.float32)
    grad_values = jnp.zeros(values_all.shape, jnp.float32)
    column_part = jnp.zeros(cumulative.shape, jnp.float32)
    grad_queries = []
    row_parts = []
    for row_start in range(0, length, block_size):
        row_end = row_start + block_size
        query_block = queries[row_start:row_end]
        grad_block = grad_attended[row_start:row_end]
        allowed = block_mask(segments[row_start:row_end], segments, row_start, block_size)
        logits = block_logits(
            query_block, keys_all, cumulative[row_start:row_end], cumulative, allowed
        )
        attn_probs = jnp.exp(logits - log_sums[:, row_start:row_end, None])
        grad_probs = jnp.einsum(
            "qhd,khd->hqk", grad_block, values_all, preferred_element_type=jnp.float32
        )
        inner = jnp.sum(attn_probs * grad_probs, axis=2, keepdims=True)
        grad_logits = to_low(attn_probs * (grad_probs - inner))
        grad_queries.append(
            jnp.einsum("hqk,khd->qhd", grad_logits, keys_all, preferred_element_type=jnp.float32)
            * qk_scale
        )
        grad_keys = (
            grad_keys
            + jnp.einsum(
                "hqk,qhd->khd", grad_logits, query_block, preferred_element_type=jnp.float32
            )
            * qk_scale
        )
        grad_values = grad_values + jnp.einsum(
            "hqk,qhd->khd", to_low(attn_probs), grad_block, preferred_element_type=jnp.float32
        )
        row_parts.append(jnp.sum(grad_logits, axis=2, dtype=jnp.float32).T)
        column_part = column_part + jnp.sum(grad_logits, axis=1, dtype=jnp.float32).T
    grad_cumul = jnp.concatenate(row_parts, axis=0) - column_part
    grad_logf = jnp.flip(jnp.cumsum(jnp.flip(grad_cumul, 0), axis=0), 0)
    return (jnp.concatenate(grad_queries, axis=0), grad_keys, grad_values, grad_logf)


def local(
    tokens,
    seg_ids,
    gain_attn,
    w_query,
    w_key,
    w_value,
    w_outgate,
    w_forget,
    forget_bias,
    w_out,
    gain_mlp,
    w_gate,
    w_up,
    w_down,
    grad_output,
):
    row_count = tokens.shape[0]
    seq_count = seg_ids.shape[0] // LEN
    tensor_parts = lax.axis_size("tensor")
    shard_parts = lax.axis_size("dp")
    gathered = (
        lax.all_gather(gain_attn, "dp", axis=0, tiled=True),
        lax.all_gather(w_query, "dp", axis=0, tiled=True),
        lax.all_gather(w_key, "dp", axis=0, tiled=True),
        lax.all_gather(w_value, "dp", axis=0, tiled=True),
        lax.all_gather(w_outgate, "dp", axis=0, tiled=True),
        lax.all_gather(w_forget, "dp", axis=0, tiled=True),
        lax.all_gather(w_out, "dp", axis=0, tiled=True),
        lax.all_gather(gain_mlp, "dp", axis=0, tiled=True),
        lax.all_gather(w_gate, "dp", axis=0, tiled=True),
        lax.all_gather(w_up, "dp", axis=0, tiled=True),
        lax.all_gather(w_down, "dp", axis=0, tiled=True),
    )
    (
        attn_gain,
        query_mat,
        key_mat,
        value_mat,
        ogate_mat,
        forget_mat,
        out_mat,
        mlp_gain,
        gate_mat,
        up_mat,
        down_mat,
    ) = gathered
    residual = tokens.astype(jnp.float32)
    unit_attn, inv_attn, normed = norm_forward(residual, attn_gain.astype(jnp.float32))
    normed_all = lax.all_gather(to_low(normed), "tensor", axis=0, tiled=True)
    query_rows = to_low(dot_plain(normed_all, query_mat))
    key_rows = to_low(dot_plain(normed_all, key_mat))
    value_rows = to_low(dot_plain(normed_all, value_mat))
    gate_pre = dot_plain(normed_all, ogate_mat)
    forget_pre = dot_plain(normed_all, forget_mat) + forget_bias.astype(jnp.float32)
    head_count = forget_mat.shape[1]
    head_size = query_mat.shape[1] // head_count
    head_shape = (seq_count, LEN, head_count, head_size)
    cumulative = jnp.cumsum(
        jax.nn.log_sigmoid(forget_pre).reshape(seq_count, LEN, head_count), axis=1
    )
    segments = seg_ids.reshape(seq_count, LEN)
    query_heads = query_rows.reshape(head_shape)
    key_heads = key_rows.reshape(head_shape)
    value_heads = value_rows.reshape(head_shape)
    attended, log_sums = lax.map(
        attend_forward, (query_heads, key_heads, value_heads, cumulative, segments)
    )
    attended = attended.reshape(seq_count * LEN, head_count * head_size)
    out_gate = jax.nn.sigmoid(gate_pre)
    gated = to_low(attended * out_gate)
    attn_terms = lax.all_to_all(
        dot_rows(gated, out_mat), "tensor", split_axis=0, concat_axis=0, tiled=True
    )
    hidden = residual + fold_parts(attn_terms, tensor_parts)
    unit_mlp, inv_mlp, normed_mlp = norm_forward(hidden, mlp_gain.astype(jnp.float32))
    normed_mlp_all = lax.all_gather(to_low(normed_mlp), "tensor", axis=0, tiled=True)
    gate_val = dot_plain(normed_mlp_all, gate_mat)
    up_val = dot_plain(normed_mlp_all, up_mat)
    sig_gate = jax.nn.sigmoid(gate_val)
    mixed = to_low(gate_val * sig_gate * up_val)
    down_terms = lax.all_to_all(
        dot_rows(mixed, down_mat).astype(jnp.bfloat16),
        "tensor",
        split_axis=0,
        concat_axis=0,
        tiled=True,
    ).astype(jnp.float32)
    output = hidden + fold_parts(down_terms, tensor_parts)
    gathered = (
        lax.all_gather(gain_attn, "dp", axis=0, tiled=True),
        lax.all_gather(w_query, "dp", axis=0, tiled=True),
        lax.all_gather(w_key, "dp", axis=0, tiled=True),
        lax.all_gather(w_value, "dp", axis=0, tiled=True),
        lax.all_gather(w_outgate, "dp", axis=0, tiled=True),
        lax.all_gather(w_forget, "dp", axis=0, tiled=True),
        lax.all_gather(w_out, "dp", axis=0, tiled=True),
        lax.all_gather(gain_mlp, "dp", axis=0, tiled=True),
        lax.all_gather(w_gate, "dp", axis=0, tiled=True),
        lax.all_gather(w_up, "dp", axis=0, tiled=True),
        lax.all_gather(w_down, "dp", axis=0, tiled=True),
    )
    (
        attn_gain,
        query_mat,
        key_mat,
        value_mat,
        ogate_mat,
        forget_mat,
        out_mat,
        mlp_gain,
        gate_mat,
        up_mat,
        down_mat,
    ) = gathered
    own_segs = lax.dynamic_slice_in_dim(seg_ids, lax.axis_index("tensor") * row_count, row_count, 0)
    grad_y = jnp.where((own_segs != 0)[:, None], grad_output, jnp.zeros_like(grad_output))
    grad_y_all = lax.all_gather(grad_y, "tensor", axis=0, tiled=True)
    grad_down = dot_cols(grad_y_all, mixed)
    grad_mixed = dot_plain(grad_y_all, down_mat)
    grad_gate = to_low(grad_mixed * up_val * sig_gate * (1.0 + gate_val * (1.0 - sig_gate)))
    grad_upval = to_low(grad_mixed * gate_val * sig_gate)
    grad_gate_mat = dot_cols(normed_mlp_all, grad_gate)
    grad_up_mat = dot_cols(normed_mlp_all, grad_upval)
    mlp_in_terms = dot_rows(grad_gate, gate_mat) + dot_rows(grad_upval, up_mat)
    grad_normed_mlp = fold_parts(
        lax.all_to_all(mlp_in_terms, "tensor", split_axis=0, concat_axis=0, tiled=True),
        tensor_parts,
    )
    back_mlp, gain_mlp_part = norm_backward(
        grad_normed_mlp, unit_mlp, inv_mlp, mlp_gain.astype(jnp.float32)
    )
    grad_hidden = grad_y.astype(jnp.float32) + back_mlp
    grad_attn_all = lax.all_gather(to_low(grad_hidden), "tensor", axis=0, tiled=True)
    grad_out_mat = dot_cols(grad_attn_all, gated)
    grad_gated = dot_plain(grad_attn_all, out_mat)
    grad_attended = to_low(grad_gated * out_gate)
    grad_gate_pre = to_low(grad_gated * attended * out_gate * (1.0 - out_gate))
    grad_q, grad_k, grad_v, grad_logf = lax.map(
        attend_backward,
        (
            query_heads,
            key_heads,
            value_heads,
            cumulative,
            segments,
            log_sums,
            grad_attended.reshape(head_shape),
        ),
    )
    flat_rows = seq_count * LEN
    grad_q = to_low(grad_q.reshape(flat_rows, head_count * head_size))
    grad_k = to_low(grad_k.reshape(flat_rows, head_count * head_size))
    grad_v = to_low(grad_v.reshape(flat_rows, head_count * head_size))
    grad_forget_pre = to_low(grad_logf.reshape(flat_rows, head_count) * jax.nn.sigmoid(-forget_pre))
    grad_query_mat = dot_cols(normed_all, grad_q)
    grad_key_mat = dot_cols(normed_all, grad_k)
    grad_value_mat = dot_cols(normed_all, grad_v)
    grad_ogate_mat = dot_cols(normed_all, grad_gate_pre)
    grad_forget_mat = dot_cols(normed_all, grad_forget_pre)
    bias_part = jnp.sum(grad_forget_pre, axis=0, dtype=jnp.float32)
    attn_in_terms = (
        dot_rows(grad_q, query_mat) + dot_rows(grad_k, key_mat) + dot_rows(grad_v, value_mat)
    )
    attn_in_terms = (
        attn_in_terms + dot_rows(grad_gate_pre, ogate_mat) + dot_rows(grad_forget_pre, forget_mat)
    )
    grad_normed_attn = fold_parts(
        lax.all_to_all(
            attn_in_terms.astype(jnp.bfloat16), "tensor", split_axis=0, concat_axis=0, tiled=True
        ).astype(attn_in_terms.dtype),
        tensor_parts,
    )
    back_attn, gain_attn_part = norm_backward(
        grad_normed_attn, unit_attn, inv_attn, attn_gain.astype(jnp.float32)
    )
    grad_tokens = to_low(grad_hidden + back_attn)
    gain_attn_sum, gain_mlp_sum = lax.psum((gain_attn_part, gain_mlp_part), "tensor")
    bias_grad = lax.psum(bias_part, "dp")
    all_recv = (
        lax.all_to_all(
            gain_attn_sum.astype(jnp.bfloat16), "dp", split_axis=0, concat_axis=0, tiled=True
        ).astype(gain_attn_sum.dtype),
        lax.all_to_all(
            grad_query_mat.astype(jnp.bfloat16), "dp", split_axis=0, concat_axis=0, tiled=True
        ).astype(grad_query_mat.dtype),
        lax.all_to_all(
            grad_key_mat.astype(jnp.bfloat16), "dp", split_axis=0, concat_axis=0, tiled=True
        ).astype(grad_key_mat.dtype),
        lax.all_to_all(
            grad_value_mat.astype(jnp.bfloat16), "dp", split_axis=0, concat_axis=0, tiled=True
        ).astype(grad_value_mat.dtype),
        lax.all_to_all(
            grad_ogate_mat.astype(jnp.bfloat16), "dp", split_axis=0, concat_axis=0, tiled=True
        ).astype(grad_ogate_mat.dtype),
        lax.all_to_all(
            grad_forget_mat.astype(jnp.bfloat16), "dp", split_axis=0, concat_axis=0, tiled=True
        ).astype(grad_forget_mat.dtype),
        lax.all_to_all(
            grad_out_mat.astype(jnp.bfloat16), "dp", split_axis=0, concat_axis=0, tiled=True
        ).astype(grad_out_mat.dtype),
        lax.all_to_all(
            gain_mlp_sum.astype(jnp.bfloat16), "dp", split_axis=0, concat_axis=0, tiled=True
        ).astype(gain_mlp_sum.dtype),
        lax.all_to_all(
            grad_gate_mat.astype(jnp.bfloat16), "dp", split_axis=0, concat_axis=0, tiled=True
        ).astype(grad_gate_mat.dtype),
        lax.all_to_all(
            grad_up_mat.astype(jnp.bfloat16), "dp", split_axis=0, concat_axis=0, tiled=True
        ).astype(grad_up_mat.dtype),
        lax.all_to_all(
            grad_down.astype(jnp.bfloat16), "dp", split_axis=0, concat_axis=0, tiled=True
        ).astype(grad_down.dtype),
    )
    sent_all = tuple((fold_parts(piece, shard_parts) for piece in all_recv))
    return (
        output.astype(jnp.bfloat16),
        grad_tokens,
        sent_all[0],
        sent_all[1],
        sent_all[2],
        sent_all[3],
        sent_all[4],
        sent_all[5],
        bias_grad,
        sent_all[6],
        sent_all[7],
        sent_all[8],
        sent_all[9],
        sent_all[10],
    )


def solution(mesh):
    placed = (
        P(("dp", "tensor"), None),
        P("dp"),
        P("dp"),
        P("dp", "tensor"),
        P("dp", "tensor"),
        P("dp", "tensor"),
        P("dp", "tensor"),
        P("dp", "tensor"),
        P("tensor"),
        P("dp", "tensor"),
        P("dp"),
        P("dp", "tensor"),
        P("dp", "tensor"),
        P("dp", "tensor"),
        P(("dp", "tensor"), None),
    )
    return jax.shard_map(
        local,
        mesh=mesh,
        in_specs=placed,
        out_specs=(
            P(("dp", "tensor"), None),
            P(("dp", "tensor"), None),
            P("dp"),
            P("dp", "tensor"),
            P("dp", "tensor"),
            P("dp", "tensor"),
            P("dp", "tensor"),
            P("dp", "tensor"),
            P("tensor"),
            P("dp", "tensor"),
            P("dp"),
            P("dp", "tensor"),
            P("dp", "tensor"),
            P("dp", "tensor"),
        ),
        check_vma=False,
    )
```

profile of v0, /device:TPU:20, one launch (start us, length us, event | category | flops | bytes accessed | tf_op | source)
XLA Modules:
  0.0 1905.0 jit_solution(4767752741099761455)
XLA Ops:
  12.7 23.6 %all-reduce.3 = (bf16[1536]{0:T(1024)(128)(2,1)S(1)}, bf16[1536]{0:T(1024)(128)(2,1)S(1)}) all-reduce(bf16[1536]{0:T(1024)(128)(2,1)S(1)} %dynamic-update-slice, bf16[1536]{0:T(1024)(128)(2,1)S(1)} %dynamic-update-slice.1), channel_id=1, replica_groups=mesh['dp'=16,'tensor'=2] {'dp'}, use_global_device_ids=true, to_apply=%add | all-reduce | flops 3072 | bytes 12288
  43.3 22.3 %all-gather = bf16[16,96,12]{1,2,0:T(8,128)(2,1)S(1)} all-gather(bf16[1,96,12]{1,2,0:T(8,128)(2,1)S(1)} %bitcast.217), channel_id=1, replica_groups=mesh['dp'=16,'tensor'=2] {'dp'}, dimensions={0}, use_global_device_ids=true | all-gather | bytes 39168 | tf_op jit(solution)/shard_map/all_gather | solution.py:165
  68.3 23.2 %all-gather.14.cloned.1.call-done = bf16[1024,1536]{1,0:T(8,128)(2,1)} async-done(((bf16[512,1536]{1,0:T(8,128)(2,1)}), bf16[1024,1536]{1,0:T(8,128)(2,1)}) %all-gather.14.cloned.1.call-update) | async-done | bytes 3145744 | tf_op jit(solution)/shard_map/all_gather | solution.py:187
  99.0 36.5 %all-gather.18.cloned.1.call-done = bf16[1536,768]{1,0:T(8,128)(2,1)} async-done(((bf16[96,768]{1,0:T(8,128)(2,1)}), bf16[1536,768]{1,0:T(8,128)(2,1)}) %all-gather.18.cloned.1.call-update) | async-done | bytes 2359312 | tf_op jit(solution)/shard_map/all_gather | solution.py:161
  141.1 37.8 %all-gather.20.cloned.1.call-done = bf16[1536,768]{1,0:T(8,128)(2,1)} async-done(((bf16[96,768]{1,0:T(8,128)(2,1)}), bf16[1536,768]{1,0:T(8,128)(2,1)}) %all-gather.20.cloned.1.call-update) | async-done | bytes 2359312 | tf_op jit(solution)/shard_map/all_gather | solution.py:162
  279.7 28.8 %all-gather.24.cloned.1.call-done = bf16[1536,768]{1,0:T(8,128)(2,1)} async-done(((bf16[96,768]{1,0:T(8,128)(2,1)}), bf16[1536,768]{1,0:T(8,128)(2,1)}) %all-gather.24.cloned.1.call-update) | async-done | bytes 2359312 | tf_op jit(solution)/shard_map/all_gather | solution.py:166
  322.7 68.8 %all-to-all-done = f32[2,512,1536]{2,1,0:T(8,128)} async-done(((f32[2,512,1536]{2,1,0:T(8,128)}), f32[2,512,1536]{2,1,0:T(8,128)}, u32[]{:S(2)}, u32[]{:S(2)}) %all-to-all-start) | async-done | bytes 6291488 | tf_op jit(solution)/shard_map/all_to_all | solution.py:209
  406.6 39.4 %all-gather.26.cloned.1.call-done = bf16[1024,1536]{1,0:T(8,128)(2,1)} async-done(((bf16[512,1536]{1,0:T(8,128)(2,1)}), bf16[1024,1536]{1,0:T(8,128)(2,1)}) %all-gather.26.cloned.1.call-update) | async-done | bytes 3145744 | tf_op jit(solution)/shard_map/all_gather | solution.py:214
  446.0 64.2 %all-gather.30.cloned.1.call-done = bf16[1536,2048]{1,0:T(8,128)(2,1)} async-done(((bf16[96,2048]{1,0:T(8,128)(2,1)}), bf16[1536,2048]{1,0:T(8,128)(2,1)}) %all-gather.30.cloned.1.call-update) | async-done | bytes 6291472 | tf_op jit(solution)/shard_map/all_gather | solution.py:169
  522.1 50.5 %all-gather.28.cloned.1.call-done = bf16[1536,2048]{1,0:T(8,128)(2,1)} async-done(((bf16[96,2048]{1,0:T(8,128)(2,1)}), bf16[1536,2048]{1,0:T(8,128)(2,1)}) %all-gather.28.cloned.1.call-update) | async-done | bytes 6291472 | tf_op jit(solution)/shard_map/all_gather | solution.py:168
  584.5 32.8 %all-gather.34.cloned.1.call-done = bf16[1024,1536]{1,0:T(8,128)(2,1)} async-done(((bf16[512,1536]{1,0:T(8,128)(2,1)}), bf16[1024,1536]{1,0:T(8,128)(2,1)}) %all-gather.34.cloned.1.call-update) | async-done | bytes 3145744 | tf_op jit(solution)/shard_map/all_gather | solution.py:255
  617.2 64.2 %all-gather.32.cloned.1.call-done = bf16[1536,2048]{1,0:T(8,128)(2,1)} async-done(((bf16[96,2048]{1,0:T(8,128)(2,1)}), bf16[1536,2048]{1,0:T(8,128)(2,1)}) %all-gather.32.cloned.1.call-update) | async-done | bytes 6291472 | tf_op jit(solution)/shard_map/all_gather | solution.py:170
  719.7 73.4 %all_to_all.137 = f32[2,512,1536]{2,1,0:T(8,128)} all-to-all(f32[2,512,1536]{2,1,0:T(8,128)S(1)} %bitcast.186), channel_id=1, replica_groups=mesh['dp'=16,'tensor'=2] {'tensor'}, dimensions={0} | all-to-all | bytes 12582912 | tf_op jit(solution)/shard_map/all_to_all | solution.py:264
  804.1 43.5 %all-gather.36.cloned.1.call-done = bf16[1024,1536]{1,0:T(8,128)(2,1)} async-done(((bf16[512,1536]{1,0:T(8,128)(2,1)}), bf16[1024,1536]{1,0:T(8,128)(2,1)}) %all-gather.36.cloned.1.call-update) | async-done | bytes 3145744 | tf_op jit(solution)/shard_map/all_gather | solution.py:271
  1018.3 22.8 %all-to-all-done.3 = bf16[2,512,1536]{2,1,0:T(8,128)(2,1)S(1)} async-done(((bf16[2,512,1536]{2,1,0:T(8,128)(2,1)}), bf16[2,512,1536]{2,1,0:T(8,128)(2,1)S(1)}, u32[]{:S(2)}, u32[]{:S(2)}) %all-to-all-start.3) | async-done | bytes 3145760 | tf_op jit(solution)/shard_map/all_to_all | solution.py:306
  1055.8 27.9 %all-to-all-done.1 = bf16[2,512,1536]{2,1,0:T(8,128)(2,1)} async-done(((bf16[2,512,1536]{2,1,0:T(8,128)(2,1)}), bf16[2,512,1536]{2,1,0:T(8,128)(2,1)}, u32[]{:S(2)}, u32[]{:S(2)}) %all-to-all-start.1) | async-done | bytes 3145760 | tf_op jit(solution)/shard_map/all_to_all | solution.py:219
  1135.5 48.0 %all-to-all-done.10 = bf16[16,96,768]{2,1,0:T(8,128)(2,1)} async-done(((bf16[16,96,768]{2,1,0:T(8,128)(2,1)}), bf16[16,96,768]{2,1,0:T(8,128)(2,1)}, u32[]{:S(2)}, u32[]{:S(2)}) %all-to-all-start.10) | async-done | bytes 2359328 | tf_op jit(solution)/shard_map/all_to_all | solution.py:336
  1193.7 47.8 %all-to-all-done.8 = bf16[16,96,768]{2,1,0:T(8,128)(2,1)} async-done(((bf16[16,96,768]{2,1,0:T(8,128)(2,1)}), bf16[16,96,768]{2,1,0:T(8,128)(2,1)}, u32[]{:S(2)}, u32[]{:S(2)}) %all-to-all-start.8) | async-done | bytes 2359328 | tf_op jit(solution)/shard_map/all_to_all | solution.py:330
  1251.5 48.0 %all-to-all-done.7 = bf16[16,96,768]{2,1,0:T(8,128)(2,1)} async-done(((bf16[16,96,768]{2,1,0:T(8,128)(2,1)}), bf16[16,96,768]{2,1,0:T(8,128)(2,1)}, u32[]{:S(2)}, u32[]{:S(2)}) %all-to-all-start.7) | async-done | bytes 2359328 | tf_op jit(solution)/shard_map/all_to_all | solution.py:327
  1309.4 48.0 %all-to-all-done.5 = bf16[16,96,768]{2,1,0:T(8,128)(2,1)} async-done(((bf16[16,96,768]{2,1,0:T(8,128)(2,1)}), bf16[16,96,768]{2,1,0:T(8,128)(2,1)}, u32[]{:S(2)}, u32[]{:S(2)}) %all-to-all-start.5) | async-done | bytes 2359328 | tf_op jit(solution)/shard_map/all_to_all | solution.py:321
  1373.2 41.9 %all-to-all-done.6 = bf16[16,96,768]{2,1,0:T(8,128)(2,1)S(1)} async-done(((bf16[16,96,768]{2,1,0:T(8,128)(2,1)}), bf16[16,96,768]{2,1,0:T(8,128)(2,1)S(1)}, u32[]{:S(2)}, u32[]{:S(2)}) %all-to-all-start.6) | async-done | bytes 2359328 | tf_op jit(solution)/shard_map/all_to_all | solution.py:324
  1432.9 126.1 %all-to-all-done.13 = bf16[16,96,2048]{2,1,0:T(8,128)(2,1)} async-done(((bf16[16,96,2048]{2,1,0:T(8,128)(2,1)}), bf16[16,96,2048]{2,1,0:T(8,128)(2,1)}, u32[]{:S(2)}, u32[]{:S(2)}) %all-to-all-start.13) | async-done | bytes 6291488 | tf_op jit(solution)/shard_map/all_to_all | solution.py:345
  1574.8 126.7 %all-to-all-done.12 = bf16[16,96,2048]{2,1,0:T(8,128)(2,1)} async-done(((bf16[16,96,2048]{2,1,0:T(8,128)(2,1)}), bf16[16,96,2048]{2,1,0:T(8,128)(2,1)}, u32[]{:S(2)}, u32[]{:S(2)}) %all-to-all-start.12) | async-done | bytes 6291488 | tf_op jit(solution)/shard_map/all_to_all | solution.py:342
  1710.7 151.6 %psum.22 = f32[12]{0:T(128)} all-reduce(f32[12]{0:T(128)S(1)} %get-tuple-element.86), channel_id=1, replica_groups=mesh['dp'=16,'tensor'=2] {'dp'}, use_global_device_ids=true, to_apply=%region_31.32 | all-reduce | flops 12 | bytes 96 | tf_op jit(solution)/shard_map/psum | solution.py:316
  (277 shorter events, 591.0 us)
Async XLA Ops:
  7.2 84.3 %all-gather.14.cloned.1.call-start = ((), (), s32[]{:S(2)}) async-start(), calls=%async_computation.15 | async-start | bytes 4718592 | tf_op jit(solution)/shard_map/all_gather | solution.py:187
  39.9 95.6 %all-gather.18.cloned.1.call-start = ((), (), s32[]{:S(2)}) async-start(), calls=%async_computation.17 | async-start | bytes 2506752 | tf_op jit(solution)/shard_map/all_gather | solution.py:161
  40.7 138.2 %all-gather.20.cloned.1.call-start = ((), (), s32[]{:S(2)}) async-start(), calls=%async_computation.18 | async-start | bytes 2506752 | tf_op jit(solution)/shard_map/all_gather | solution.py:162
  41.4 180.7 %all-gather.16.cloned.1.call-start = ((), (), s32[]{:S(2)}) async-start(), calls=%async_computation.16 | async-start | bytes 2506752 | tf_op jit(solution)/shard_map/all_gather | solution.py:163
  42.0 230.8 %all-gather.22.cloned.1.call-start = ((), (), s32[]{:S(2)}) async-start(), calls=%async_computation.19 | async-start | bytes 2506752 | tf_op jit(solution)/shard_map/all_gather | solution.py:164
  42.6 265.9 %all-gather.24.cloned.1.call-start = ((), (), s32[]{:S(2)}) async-start(), calls=%async_computation.20 | async-start | bytes 2506752 | tf_op jit(solution)/shard_map/all_gather | solution.py:166
  315.9 75.6 %all-to-all-start = ((f32[2,512,1536]{2,1,0:T(8,128)}), f32[2,512,1536]{2,1,0:T(8,128)}, u32[]{:S(2)}, u32[]{:S(2)}) async-start(f32[2,512,1536]{2,1,0:T(8,128)} %bitcast.185), calls=%async_computation | async-start | bytes 12582912 | tf_op jit(solution)/shard_map/all_to_all | solution.py:209
  322.7 123.3 %all-gather.26.cloned.1.call-start = ((), (), s32[]{:S(2)}) async-start(), calls=%async_computation.21 | async-start | bytes 4718592 | tf_op jit(solution)/shard_map/all_gather | solution.py:214
  401.5 108.8 %all-gather.30.cloned.1.call-start = ((), (), s32[]{:S(2)}) async-start(), calls=%async_computation.23 | async-start | bytes 6684672 | tf_op jit(solution)/shard_map/all_gather | solution.py:169
  402.2 170.5 %all-gather.28.cloned.1.call-start = ((), (), s32[]{:S(2)}) async-start(), calls=%async_computation.22 | async-start | bytes 6684672 | tf_op jit(solution)/shard_map/all_gather | solution.py:168
  402.9 214.3 %all-gather.34.cloned.1.call-start = ((), (), s32[]{:S(2)}) async-start(), calls=%async_computation.25 | async-start | bytes 4718592 | tf_op jit(solution)/shard_map/all_gather | solution.py:255
  405.8 275.6 %all-gather.32.cloned.1.call-start = ((), (), s32[]{:S(2)}) async-start(), calls=%async_computation.24 | async-start | bytes 6684672 | tf_op jit(solution)/shard_map/all_gather | solution.py:170
  406.6 441.0 %all-gather.36.cloned.1.call-start = ((), (), s32[]{:S(2)}) async-start(), calls=%async_computation.26 | async-start | bytes 4718592 | tf_op jit(solution)/shard_map/all_gather | solution.py:271
  1001.2 39.9 %all-to-all-start.3 = ((bf16[2,512,1536]{2,1,0:T(8,128)(2,1)}), bf16[2,512,1536]{2,1,0:T(8,128)(2,1)S(1)}, u32[]{:S(2)}, u32[]{:S(2)}) async-start(bf16[2,512,1536]{2,1,0:T(8,128)(2,1)} %bitcast.38), calls=%async_computation.3 | async-start | bytes 6291456 | tf_op jit(solution)/shard_map/all_to_all | solution.py:306
  1042.7 40.9 %all-to-all-start.1 = ((bf16[2,512,1536]{2,1,0:T(8,128)(2,1)}), bf16[2,512,1536]{2,1,0:T(8,128)(2,1)}, u32[]{:S(2)}, u32[]{:S(2)}) async-start(bf16[2,512,1536]{2,1,0:T(8,128)(2,1)} %bitcast.193), calls=%async_computation.1 | async-start | bytes 6291456 | tf_op jit(solution)/shard_map/all_to_all | solution.py:219
  1083.7 17.9 all-to-all-start.9
  1123.8 59.7 %all-to-all-start.10 = ((bf16[16,96,768]{2,1,0:T(8,128)(2,1)}), bf16[16,96,768]{2,1,0:T(8,128)(2,1)}, u32[]{:S(2)}, u32[]{:S(2)}) async-start(bf16[16,96,768]{2,1,0:T(8,128)(2,1)} %bitcast.194), calls=%async_computation.10 | async-start | bytes 4718592 | tf_op jit(solution)/shard_map/all_to_all | solution.py:336
  1183.4 58.1 %all-to-all-start.8 = ((bf16[16,96,768]{2,1,0:T(8,128)(2,1)}), bf16[16,96,768]{2,1,0:T(8,128)(2,1)}, u32[]{:S(2)}, u32[]{:S(2)}) async-start(bf16[16,96,768]{2,1,0:T(8,128)(2,1)} %bitcast.197), calls=%async_computation.8 | async-start | bytes 4718592 | tf_op jit(solution)/shard_map/all_to_all | solution.py:330
  1241.5 57.9 %all-to-all-start.7 = ((bf16[16,96,768]{2,1,0:T(8,128)(2,1)}), bf16[16,96,768]{2,1,0:T(8,128)(2,1)}, u32[]{:S(2)}, u32[]{:S(2)}) async-start(bf16[16,96,768]{2,1,0:T(8,128)(2,1)} %bitcast.198), calls=%async_computation.7 | async-start | bytes 4718592 | tf_op jit(solution)/shard_map/all_to_all | solution.py:327
  1299.4 57.9 %all-to-all-start.5 = ((bf16[16,96,768]{2,1,0:T(8,128)(2,1)}), bf16[16,96,768]{2,1,0:T(8,128)(2,1)}, u32[]{:S(2)}, u32[]{:S(2)}) async-start(bf16[16,96,768]{2,1,0:T(8,128)(2,1)} %bitcast.195), calls=%async_computation.5 | async-start | bytes 4718592 | tf_op jit(solution)/shard_map/all_to_all | solution.py:321
  1357.4 57.8 %all-to-all-start.6 = ((bf16[16,96,768]{2,1,0:T(8,128)(2,1)}), bf16[16,96,768]{2,1,0:T(8,128)(2,1)S(1)}, u32[]{:S(2)}, u32[]{:S(2)}) async-start(bf16[16,96,768]{2,1,0:T(8,128)(2,1)} %bitcast.196), calls=%async_computation.6 | async-start | bytes 4718592 | tf_op jit(solution)/shard_map/all_to_all | solution.py:324
  1416.7 142.4 %all-to-all-start.13 = ((bf16[16,96,2048]{2,1,0:T(8,128)(2,1)}), bf16[16,96,2048]{2,1,0:T(8,128)(2,1)}, u32[]{:S(2)}, u32[]{:S(2)}) async-start(bf16[16,96,2048]{2,1,0:T(8,128)(2,1)} %bitcast.184), calls=%async_computation.13 | async-start | bytes 12582912 | tf_op jit(solution)/shard_map/all_to_all | solution.py:345
  1559.0 142.4 %all-to-all-start.12 = ((bf16[16,96,2048]{2,1,0:T(8,128)(2,1)}), bf16[16,96,2048]{2,1,0:T(8,128)(2,1)}, u32[]{:S(2)}, u32[]{:S(2)}) async-start(bf16[16,96,2048]{2,1,0:T(8,128)(2,1)} %bitcast.183), calls=%async_computation.12 | async-start | bytes 12582912 | tf_op jit(solution)/shard_map/all_to_all | solution.py:342
  1701.5 191.2 %all-to-all-start.14 = ((bf16[16,96,2048]{2,1,0:T(8,128)(2,1)}), bf16[16,96,2048]{2,1,0:T(8,128)(2,1)}, u32[]{:S(2)}, u32[]{:S(2)}) async-start(bf16[16,96,2048]{2,1,0:T(8,128)(2,1)} %bitcast.182), calls=%async_computation.14 | async-start | bytes 12582912 | tf_op jit(solution)/shard_map/all_to_all | solution.py:348
  (56 other events, 3124.8 us)
Sparse Core Ops, SparseCore 0:
  40.1 51.3 all-gather.13
  93.7 41.7 all-gather.17
  137.9 41.0 all-gather.19
  181.1 41.0 all-gather.15
  224.3 41.0 all-gather.21
  267.5 41.0 all-gather.23
  401.6 44.4 all-gather.25
  448.3 61.8 all-gather.29
  512.5 60.0 all-gather.27
  574.1 43.1 all-gather.33
  619.5 61.8 all-gather.31
  804.1 43.3 all-gather.35
where the time goes:
time: 1920 us; the launch traced here: 1910 us
  waiting for transfers between devices  1050 us (55%)
  matrix products  320 us (17%)
  blocking collectives  279 us (15%)
  other arithmetic  147 us (8%)
  starting transfers between devices  77 us (4%)
    psum x1, blocking collectives, local(): bias_grad = lax.psum(bias_part, 'dp')  152 us
    all_to_all x1, waiting for transfers between devices, local(): lax.all_to_all(grad_gate_mat.astype(jnp.bfloat16), 'dp', split_axis=0, co...  127 us
    all_to_all x1, waiting for transfers between devices, local(): lax.all_to_all(grad_up_mat.astype(jnp.bfloat16), 'dp', split_axis=0, conc...  126 us
    dot_general x9, matrix products, dot_plain(): return jnp.dot(left, right, preferred_element_type=jnp.float32)  75 us
    all_to_all x1, blocking collectives, local(): lax.all_to_all(mlp_in_terms, 'tensor', split_axis=0, concat_axis=0, tiled...  73.4 us
    all_to_all x1, waiting for transfers between devices, local(): lax.all_to_all(dot_rows(gated, out_mat), 'tensor', split_axis=0, concat_a...  68.8 us
    all_gather x1, waiting for transfers between devices, local(): lax.all_gather(w_down, 'dp', axis=0, tiled=True)  64.2 us
    all_gather x1, waiting for transfers between devices, local(): lax.all_gather(w_up, 'dp', axis=0, tiled=True)  64.2 us
  transfers between devices with their start and end apart: 26, of which 22 were waited for; matrix products, arithmetic and copies ran while one was open for 13% of the time, Pallas kernels for 0%

commit v1 on v0

v1 whole, which is shorter than its diff:
```python
import functools

import jax
import jax.numpy as jnp
from jax import lax
from jax.experimental import pallas as pl
from jax.experimental.pallas import tpu as pltpu
from jax.sharding import PartitionSpec as P

LEN = 1024
epsilon = 1e-06


NEG = -1e30


def lane_split(value, head):
    lanes = lax.broadcasted_iota(jnp.int32, value.shape, 1)
    return lanes < 64 if head == 0 else lanes >= 64


def dot_nt(left, right):
    return lax.dot_general(
        left, right, (((1,), (1,)), ((), ())), preferred_element_type=jnp.float32
    )


def dot_tn(left, right):
    return lax.dot_general(
        left, right, (((0,), (0,)), ((), ())), preferred_element_type=jnp.float32
    )


def tile_allowed(start_row, height, first, width):
    key_pos = lax.broadcasted_iota(jnp.int32, (height, width), 0)
    query_pos = first + lax.broadcasted_iota(jnp.int32, (height, width), 1)
    return (key_pos >= start_row) & (key_pos <= query_pos)


def attend_forward_kernel(block, q_ref, k_ref, v_ref, ccol_ref, crow_ref, start_ref, o_ref, lse_ref):
    length = q_ref.shape[0]
    scale = jnp.asarray(0.125, jnp.bfloat16)
    for first in range(0, length, block):
        height = first + block
        query = q_ref[first : first + block, :] * scale
        start_row = start_ref[0, :, first : first + block]
        keys_all = k_ref[:height, :]
        values_all = v_ref[:height, :]
        outs = []
        for head in range(2):
            keys = jnp.where(lane_split(keys_all, head), keys_all, jnp.zeros_like(keys_all))
            logits = dot_nt(keys, query)
            logits = (logits + crow_ref[0, head : head + 1, first : first + block]) - ccol_ref[
                0, :height, head : head + 1
            ]
            logits = jnp.where(tile_allowed(start_row, height, first, block), logits, NEG)
            largest = jnp.max(logits, axis=0, keepdims=True)
            exponent = jnp.exp(logits - largest)
            total = jnp.sum(exponent, axis=0, keepdims=True)
            probs = (exponent * (1.0 / total)).astype(jnp.bfloat16)
            lse_ref[0, head : head + 1, first : first + block] = largest + jnp.log(total)
            outs.append(dot_tn(values_all, probs))
        rows = lax.broadcasted_iota(jnp.int32, outs[0].shape, 0)
        both = jnp.where(rows < 64, outs[0], outs[1])
        o_ref[first : first + block, :] = both.T


def attend_backward_kernel(
    block,
    q_ref,
    k_ref,
    v_ref,
    g_ref,
    ccol_ref,
    crow_ref,
    lse_ref,
    start_ref,
    dq_ref,
    dk_ref,
    dv_ref,
    row_ref,
    col_ref,
    dk_acc,
    dv_acc,
):
    length = q_ref.shape[0]
    scale = jnp.asarray(0.125, jnp.bfloat16)
    for first in reversed(range(0, length, block)):
        height = first + block
        top = height == length
        query = q_ref[first : first + block, :] * scale
        grad = g_ref[first : first + block, :]
        start_row = start_ref[0, :, first : first + block]
        keys_all = k_ref[:height, :]
        values_all = v_ref[:height, :]
        zeros = jnp.zeros_like(keys_all)
        outs = []
        for head in range(2):
            own = lane_split(keys_all, head)
            logits = dot_nt(jnp.where(own, keys_all, zeros), query)
            shift = (
                crow_ref[0, head : head + 1, first : first + block]
                - lse_ref[0, head : head + 1, first : first + block]
            )
            logits = (logits + shift) - ccol_ref[0, :height, head : head + 1]
            allowed = tile_allowed(start_row, height, first, block)
            probs = jnp.where(allowed, jnp.exp(logits), 0.0)
            grad_probs = dot_nt(jnp.where(own, values_all, zeros), grad)
            inner = jnp.sum(probs * grad_probs, axis=0, keepdims=True)
            grad_logits = (probs * (grad_probs - inner)).astype(jnp.bfloat16)
            low_probs = probs.astype(jnp.bfloat16)
            query_own = lane_split(query, head)
            one_query = jnp.where(query_own, query, jnp.ones_like(query))
            dk_part = jnp.dot(grad_logits, one_query, preferred_element_type=jnp.float32)
            dv_part = jnp.dot(low_probs, grad, preferred_element_type=jnp.float32)
            if top:
                dk_acc[head] = dk_part
                dv_acc[head] = dv_part
            else:
                dk_acc[head, :height, :] += dk_part
                dv_acc[head, :height, :] += dv_part
            out = dot_tn(jnp.where(own, keys_all, jnp.ones_like(keys_all)), grad_logits)
            other = 64 - 64 * head
            row_ref[0, head : head + 1, first : first + block] = out[other : other + 1, :]
            outs.append(out)
        rows = lax.broadcasted_iota(jnp.int32, outs[0].shape, 0)
        both = jnp.where(rows < 64, outs[0], outs[1]) * 0.125
        dq_ref[first : first + block, :] = both.T.astype(jnp.bfloat16)
    first_half = lane_split(dk_acc[0], 0)
    dk_ref[...] = jnp.where(first_half, dk_acc[0], dk_acc[1]).astype(jnp.bfloat16)
    dv_ref[...] = jnp.where(first_half, dv_acc[0], dv_acc[1]).astype(jnp.bfloat16)
    col_ref[0, :, 0:1] = dk_acc[0, :, 64:65]
    col_ref[0, :, 1:2] = dk_acc[1, :, 0:1]


def attention_specs(length, pairs):
    wide = pl.BlockSpec((length, 128), lambda s, p: (s, p))
    column = pl.BlockSpec((1, length, 2), lambda s, p: (s * pairs + p, 0, 0))
    row = pl.BlockSpec((1, 2, length), lambda s, p: (s * pairs + p, 0, 0))
    start = pl.BlockSpec((1, 1, length), lambda s, p: (s, 0, 0))
    return wide, column, row, start


def attend_forward(queries, keys, values, ccol, crow, start):
    seqs, _, length = start.shape
    pairs = queries.shape[1] // 128
    wide, column, row, first = attention_specs(length, pairs)
    tiles = seqs * pairs
    cost = pl.CostEstimate(
        flops=tiles * length * length * 512, bytes_accessed=queries.size * 10, transcendentals=tiles * length * length
    )
    return pl.pallas_call(
        functools.partial(attend_forward_kernel, min(256, length)),
        grid=(seqs, pairs),
        in_specs=[wide, wide, wide, column, row, first],
        out_specs=[wide, row],
        out_shape=[
            jax.ShapeDtypeStruct(queries.shape, jnp.float32),
            jax.ShapeDtypeStruct((tiles, 2, length), jnp.float32),
        ],
        compiler_params=pltpu.CompilerParams(vmem_limit_bytes=48 << 20),
        cost_estimate=cost,
        name="attend_forward",
    )(queries, keys, values, ccol, crow, start)


def attend_backward(queries, keys, values, grad, ccol, crow, lse, start):
    seqs, _, length = start.shape
    pairs = queries.shape[1] // 128
    wide, column, row, first = attention_specs(length, pairs)
    tiles = seqs * pairs
    cost = pl.CostEstimate(
        flops=tiles * length * length * 1280, bytes_accessed=queries.size * 14, transcendentals=tiles * length * length
    )
    low = jax.ShapeDtypeStruct(queries.shape, jnp.bfloat16)
    return pl.pallas_call(
        functools.partial(attend_backward_kernel, min(256, length)),
        grid=(seqs, pairs),
        in_specs=[wide, wide, wide, wide, column, row, row, first],
        out_specs=[wide, wide, wide, row, column],
        out_shape=[
            low,
            low,
            low,
            jax.ShapeDtypeStruct((tiles, 2, length), jnp.float32),
            jax.ShapeDtypeStruct((tiles, length, 2), jnp.float32),
        ],
        scratch_shapes=[
            pltpu.VMEM((2, length, 128), jnp.float32),
            pltpu.VMEM((2, length, 128), jnp.float32),
        ],
        compiler_params=pltpu.CompilerParams(vmem_limit_bytes=48 << 20),
        cost_estimate=cost,
        name="attend_backward",
    )(queries, keys, values, grad, ccol, crow, lse, start)


def to_low(value):
    return value.astype(jnp.bfloat16)


def dot_plain(left, right):
    return jnp.dot(left, right, preferred_element_type=jnp.float32)


dot_rows = dot_nt
dot_cols = dot_tn


def norm_forward(values, gain):
    inverse = lax.rsqrt(jnp.mean(values * values, axis=-1, keepdims=True) + epsilon)
    unit_rows = values * inverse
    return (unit_rows, inverse, unit_rows * gain)


def norm_backward(grad_normed, unit_rows, inverse, gain):
    grad_unit = grad_normed * gain
    centred = grad_unit - unit_rows * jnp.mean(grad_unit * unit_rows, axis=-1, keepdims=True)
    return (inverse * centred, jnp.sum(grad_normed * unit_rows, axis=0))


SWAP = [(0, 1), (1, 0)]


def join_halves(own, side):
    other = lax.ppermute(own, "tensor", SWAP)
    first = jnp.where(side == 0, own, other)
    second = jnp.where(side == 0, other, own)
    return jnp.concatenate([first, second], axis=0)


def sum_halves(terms, side):
    rows = terms.shape[0] // 2
    away = lax.dynamic_slice_in_dim(terms, (1 - side) * rows, rows, 0)
    arrived = lax.ppermute(to_low(away), "tensor", SWAP)
    return lax.dynamic_slice_in_dim(terms, side * rows, rows, 0) + arrived.astype(jnp.float32)


def document_starts(segments):
    position = jnp.arange(segments.shape[-1], dtype=jnp.int32)
    before = (segments[..., None, :] != segments[..., :, None]) & (position[None, :] < position[:, None])
    starts = jnp.sum(before, axis=-1, dtype=jnp.int32)
    return jnp.where(segments != 0, starts, position)


def local(
    tokens,
    seg_ids,
    gain_attn,
    w_query,
    w_key,
    w_value,
    w_outgate,
    w_forget,
    forget_bias,
    w_out,
    gain_mlp,
    w_gate,
    w_up,
    w_down,
    grad_output,
):
    row_count, width = tokens.shape
    seq_count = seg_ids.shape[0] // LEN
    side = lax.axis_index("tensor")
    cols = w_query.shape[1]
    head_count = w_forget.shape[1]
    hidden_cols = w_gate.shape[1]
    pad = 128 - head_count - 2
    packed = jnp.concatenate(
        [
            w_query,
            w_key,
            w_value,
            w_outgate,
            w_forget,
            gain_attn[:, None],
            gain_mlp[:, None],
            jnp.zeros((w_query.shape[0], pad), jnp.bfloat16),
        ],
        axis=1,
    )
    attn_mat = lax.all_gather(packed, "dp", axis=0, tiled=True)
    rest = jnp.concatenate([w_out, w_gate, w_up, w_down], axis=1)
    rest_mat = lax.all_gather(rest, "dp", axis=0, tiled=True)
    out_mat = rest_mat[:, :cols]
    gate_mat = rest_mat[:, cols : cols + hidden_cols]
    up_mat = rest_mat[:, cols + hidden_cols : cols + 2 * hidden_cols]
    down_mat = rest_mat[:, cols + 2 * hidden_cols :]
    gains = attn_mat[:, 4 * cols + head_count : 4 * cols + head_count + 2].astype(jnp.float32).T
    attn_gain, mlp_gain = gains[0], gains[1]

    residual = tokens.astype(jnp.float32)
    unit_attn, inv_attn, normed = norm_forward(residual, attn_gain)
    normed_all = join_halves(to_low(normed), side)
    query_rows = to_low(dot_plain(normed_all, attn_mat[:, :cols]))
    key_rows = to_low(dot_plain(normed_all, attn_mat[:, cols : 2 * cols]))
    value_rows = to_low(dot_plain(normed_all, attn_mat[:, 2 * cols : 3 * cols]))
    gate_pre = dot_plain(normed_all, attn_mat[:, 3 * cols : 4 * cols])
    forget_pre = dot_plain(normed_all, attn_mat[:, 4 * cols :])[:, :head_count] + forget_bias.astype(
        jnp.float32
    )
    cumulative = jnp.cumsum(
        jax.nn.log_sigmoid(forget_pre).reshape(seq_count, LEN, head_count), axis=1
    )
    pairs = head_count // 2
    tiles = seq_count * pairs
    paired = cumulative.reshape(seq_count, LEN, pairs, 2)
    ccol = paired.transpose(0, 2, 1, 3).reshape(tiles, LEN, 2)
    crow = paired.transpose(0, 2, 3, 1).reshape(tiles, 2, LEN)
    start = document_starts(seg_ids.reshape(seq_count, LEN))[:, None, :]
    attended, lse = attend_forward(query_rows, key_rows, value_rows, ccol, crow, start)
    out_gate = jax.nn.sigmoid(gate_pre)
    gated = to_low(attended * out_gate)
    hidden = residual + sum_halves(dot_rows(gated, out_mat), side)
    unit_mlp, inv_mlp, normed_mlp = norm_forward(hidden, mlp_gain)
    normed_mlp_all = join_halves(to_low(normed_mlp), side)
    gate_val = dot_plain(normed_mlp_all, gate_mat)
    up_val = dot_plain(normed_mlp_all, up_mat)
    sig_gate = jax.nn.sigmoid(gate_val)
    mixed = to_low(gate_val * sig_gate * up_val)
    output = hidden + sum_halves(dot_rows(mixed, down_mat), side)

    own_segs = lax.dynamic_slice_in_dim(seg_ids, side * row_count, row_count, 0)
    grad_y = jnp.where((own_segs != 0)[:, None], grad_output, jnp.zeros_like(grad_output))
    grad_y_all = join_halves(grad_y, side)
    grad_down = to_low(dot_cols(grad_y_all, mixed))
    grad_mixed = dot_plain(grad_y_all, down_mat)
    grad_gate = to_low(grad_mixed * up_val * sig_gate * (1.0 + gate_val * (1.0 - sig_gate)))
    grad_upval = to_low(grad_mixed * gate_val * sig_gate)
    grad_gate_mat = to_low(dot_cols(normed_mlp_all, grad_gate))
    grad_up_mat = to_low(dot_cols(normed_mlp_all, grad_upval))
    mlp_grads = jnp.concatenate([grad_gate_mat, grad_up_mat, grad_down], axis=1)
    mlp_sent = lax.psum_scatter(mlp_grads, "dp", scatter_dimension=0, tiled=True)
    mlp_in_terms = dot_rows(grad_gate, gate_mat) + dot_rows(grad_upval, up_mat)
    grad_normed_mlp = sum_halves(mlp_in_terms, side)
    back_mlp, gain_mlp_part = norm_backward(grad_normed_mlp, unit_mlp, inv_mlp, mlp_gain)
    grad_hidden = grad_y.astype(jnp.float32) + back_mlp
    grad_attn_all = join_halves(to_low(grad_hidden), side)
    grad_out_mat = to_low(dot_cols(grad_attn_all, gated))
    grad_gated = dot_plain(grad_attn_all, out_mat)
    grad_attended = to_low(grad_gated * out_gate)
    grad_gate_pre = to_low(grad_gated * attended * out_gate * (1.0 - out_gate))
    grad_q, grad_k, grad_v, row_part, col_part = attend_backward(
        query_rows, key_rows, value_rows, grad_attended, ccol, crow, lse, start
    )
    flat_rows = seq_count * LEN
    grad_cumul = row_part.reshape(seq_count, pairs, 2, LEN).transpose(0, 3, 1, 2) - col_part.reshape(
        seq_count, pairs, LEN, 2
    ).transpose(0, 2, 1, 3)
    grad_cumul = grad_cumul.reshape(seq_count, LEN, head_count)
    grad_logf = jnp.flip(jnp.cumsum(jnp.flip(grad_cumul, 1), axis=1), 1)
    grad_forget_pre = to_low(grad_logf.reshape(flat_rows, head_count) * jax.nn.sigmoid(-forget_pre))
    forget_pad = jnp.pad(grad_forget_pre, ((0, 0), (0, 128 - head_count)))
    grad_parts = (grad_q, grad_k, grad_v, grad_gate_pre, forget_pad)
    attn_grads = jnp.concatenate(
        [grad_out_mat] + [to_low(dot_cols(normed_all, part)) for part in grad_parts], axis=1
    )
    attn_sent = lax.psum_scatter(attn_grads, "dp", scatter_dimension=0, tiled=True)
    bias_part = jnp.sum(grad_forget_pre, axis=0, dtype=jnp.float32)
    attn_in_terms = dot_rows(jnp.concatenate(grad_parts, axis=1), attn_mat)
    grad_normed_attn = sum_halves(attn_in_terms, side)
    back_attn, gain_attn_part = norm_backward(grad_normed_attn, unit_attn, inv_attn, attn_gain)
    grad_tokens = to_low(grad_hidden + back_attn)
    slots = lax.dynamic_update_slice_in_dim(
        jnp.zeros((lax.axis_size("tensor") * head_count,), jnp.float32), bias_part, side * head_count, 0
    )
    small = lax.psum(jnp.concatenate([gain_attn_part, gain_mlp_part, slots]), ("dp", "tensor"))
    own = gain_attn.shape[0]
    at = lax.axis_index("dp") * own
    gain_attn_grad = lax.dynamic_slice_in_dim(small, at, own, 0)
    gain_mlp_grad = lax.dynamic_slice_in_dim(small, width + at, own, 0)
    bias_grad = lax.dynamic_slice_in_dim(small, 2 * width + side * head_count, head_count, 0)
    attn_sent = attn_sent.astype(jnp.float32)
    mlp_sent = mlp_sent.astype(jnp.float32)
    return (
        to_low(output),
        grad_tokens,
        gain_attn_grad,
        attn_sent[:, cols : 2 * cols],
        attn_sent[:, 2 * cols : 3 * cols],
        attn_sent[:, 3 * cols : 4 * cols],
        attn_sent[:, 4 * cols : 5 * cols],
        attn_sent[:, 5 * cols : 5 * cols + head_count],
        bias_grad,
        attn_sent[:, :cols],
        gain_mlp_grad,
        mlp_sent[:, :hidden_cols],
        mlp_sent[:, hidden_cols : 2 * hidden_cols],
        mlp_sent[:, 2 * hidden_cols :],
    )


def solution(mesh):
    placed = (
        P(("dp", "tensor"), None),
        P("dp"),
        P("dp"),
        P("dp", "tensor"),
        P("dp", "tensor"),
        P("dp", "tensor"),
        P("dp", "tensor"),
        P("dp", "tensor"),
        P("tensor"),
        P("dp", "tensor"),
        P("dp"),
        P("dp", "tensor"),
        P("dp", "tensor"),
        P("dp", "tensor"),
        P(("dp", "tensor"), None),
    )
    return jax.shard_map(
        local,
        mesh=mesh,
        in_specs=placed,
        out_specs=(
            P(("dp", "tensor"), None),
            P(("dp", "tensor"), None),
            P("dp"),
            P("dp", "tensor"),
            P("dp", "tensor"),
            P("dp", "tensor"),
            P("dp", "tensor"),
            P("dp", "tensor"),
            P("tensor"),
            P("dp", "tensor"),
            P("dp"),
            P("dp", "tensor"),
            P("dp", "tensor"),
            P("dp", "tensor"),
        ),
        check_vma=False,
    )
```

time: 1920 us -> 907 us (0.47)
  waiting for transfers between devices: 1050 us -> 467 us
  blocking collectives: 279 us -> 42.7 us
  matrix products: 320 us -> 174 us
  other arithmetic: 147 us -> 60.6 us
  Pallas kernels: 0 us -> 70.5 us
  starting transfers between devices: 77 us -> 6.61 us
  local copies, waits for them, and re-layouts: 14.3 us -> 63.5 us
    all_to_all x14 -> x0, waiting for transfers between devices: 609 us -> none  [the longest x1 127 us: local(): lax.all_to_all(grad_gate_mat.astype(jnp.bfloat16), 'dp', split_axis=0, co...]
    all_gather x12 -> x2, waiting for transfers between devices: 437 us -> 82.3 us  [the longest x1 80.8 us: local(): attn_mat = lax.all_gather(packed, 'dp', axis=0, tiled=True)]
    ppermute x0 -> x8, waiting for transfers between devices: none -> 211 us  [the longest x4 121 us: sum_halves(): arrived = lax.ppermute(to_low(away), 'tensor', SWAP)]
    reduce_scatter x0 -> x1, waiting for transfers between devices: none -> 173 us  [local(): lax.psum_scatter(mlp_grads, 'dp', scatter_dimension=0, tiled=True)]
    dot_general x30 -> x14, matrix products: 245 us -> 100 us  [the longest x9 50.8 us: dot_tn(): lax.dot_general(left, right, (((0,), (0,)), ((), ())), preferred_element_...]
    psum x2 -> x1, blocking collectives: 160 us -> 42.7 us  [local(): lax.psum(jnp.concatenate([gain_attn_part, gain_mlp_part, slots]), ('dp',...]
    reduce_sum x19 -> x1, other arithmetic: 106 us -> 0.52 us  [document_starts(): starts = jnp.sum(before, axis=-1, dtype=jnp.int32)]
    all_to_all x14 -> x0, starting transfers between devices: 76.6 us -> none  [the longest x1 7.24 us: local(): lax.all_to_all(dot_rows(mixed, down_mat).astype(jnp.bfloat16), 'tensor',...]
  transfers between devices with their start and end apart: 26 -> 12, of which waited for: 22 -> 10; matrix products, arithmetic and copies ran while one was open for 13% -> 17% of each run, Pallas kernels for 0% -> 4%
where the time goes in v1:
time: 907 us; the launch traced here: 899 us
  waiting for transfers between devices  467 us (51%)
  matrix products  174 us (19%)
  Pallas kernels  70.5 us (8%)
  local copies, waits for them, and re-layouts  63.5 us (7%)
  other arithmetic  60.6 us (7%)
  blocking collectives  42.7 us (5%)
  between operations  14.6 us (2%)
    reduce_scatter x1, waiting for transfers between devices, local(): lax.psum_scatter(mlp_grads, 'dp', scatter_dimension=0, tiled=True)  173 us
    ppermute x4, waiting for transfers between devices, sum_halves(): arrived = lax.ppermute(to_low(away), 'tensor', SWAP)  121 us
    ppermute x4, waiting for transfers between devices, join_halves(): other = lax.ppermute(own, 'tensor', SWAP)  90 us
    all_gather x1, waiting for transfers between devices, local(): attn_mat = lax.all_gather(packed, 'dp', axis=0, tiled=True)  80.8 us
    dot_general x9, matrix products, dot_plain(): return jnp.dot(left, right, preferred_element_type=jnp.float32)  73.8 us
    dot_general x9, matrix products, dot_tn(): lax.dot_general(left, right, (((0,), (0,)), ((), ())), preferred_element_...  50.8 us
    dot_general x5, matrix products, dot_nt(): lax.dot_general(left, right, (((1,), (1,)), ((), ())), preferred_element_...  49.5 us
    psum x1, blocking collectives, local(): lax.psum(jnp.concatenate([gain_attn_part, gain_mlp_part, slots]), ('dp',...  42.7 us
  transfers between devices with their start and end apart: 12, of which 10 were waited for; matrix products, arithmetic and copies ran while one was open for 17% of the time, Pallas kernels for 4%

profile of v1, /device:TPU:20, one launch (start us, length us, event | category | flops | bytes accessed | tf_op | source)
XLA Modules:
  0.0 899.2 jit_solution(5058812673045547476)
XLA Ops:
  14.6 80.8 %all-gather.3.cloned.1.call-done = bf16[1536,3200]{1,0:T(8,128)(2,1)} async-done(((bf16[96,3200]{1,0:T(8,128)(2,1)}), bf16[1536,3200]{1,0:T(8,128)(2,1)}) %all-gather.3.cloned.1.call-update) | async-done | bytes 9830416 | tf_op jit(solution)/shard_map/all_gather | solution.py:283
  104.3 32.2 %collective-permute-done = bf16[512,1536]{1,0:T(8,128)(2,1)} collective-permute-done((bf16[512,1536]{1,0:T(8,128)(2,1)}, bf16[512,1536]{1,0:T(8,128)(2,1)}, u32[]{:S(2)}, u32[]{:S(2)}) %collective-permute-start) | collective-permute-done | bytes 1572896 | tf_op jit(solution)/shard_map/ppermute | solution.py:226
  164.1 32.8 %attend_forward.1 = (f32[1024,768]{1,0:T(8,128)}, f32[6,2,1024]{2,1,0:T(2,128)S(1)}) custom-call(bf16[1024,768]{1,0:T(8,128)(2,1)S(1)} %fusion.46.q_ref, bf16[1024,768]{1,0:T(8,128)(2,1)S(1)} %fusion.49.k_ref, bf16[1024,768]{1,0:T(8,128)(2,1)S(1)} %fusion.52.v_ref, f32[6,1024,2]{2,1,0:T(8,128)} %bitcast.72, f32[6,2,1024]{2,1,0:T(2,128)S(1)} %bitcast.68, ...), custom_call_target="tpu_custom_call" | custom-call | flops 3221225472 | bytes 7864320 | tf_op jit(solution)/shard_map/attend_forward/pallas_call | solution.py:152
  196.9 7.9 multiply_convert_fusion.6
  214.1 33.7 %collective-permute-done.1 = bf16[512,1536]{1,0:T(8,128)(2,1)S(1)} collective-permute-done((bf16[512,1536]{1,0:T(8,128)(2,1)S(1)}, bf16[512,1536]{1,0:T(8,128)(2,1)S(1)}, u32[]{:S(2)}, u32[]{:S(2)}) %collective-permute-start.1) | collective-permute-done | bytes 1572896 | tf_op jit(solution)/shard_map/ppermute | solution.py:235
  249.5 10.8 %fusion = f32[1024,2048]{1,0:T(8,128)} fusion(bf16[1536,6912]{1,0:T(8,128)(2,1)} %all-gather.5.cloned.1.call-done, bf16[512,1536]{1,0:T(8,128)(2,1)S(1)} %get-tuple-element.119, bf16[512,1536]{1,0:T(8,128)(2,1)S(1)} %get-tuple-element.118), kind=kOutput, calls=%fused_computation.8 | convolution fusion | flops 6448742400 | bytes 17825792 | tf_op jit(solution)/shard_map/dot_general | solution.py:203
  260.4 24.3 %collective-permute-done.2 = bf16[512,1536]{1,0:T(8,128)(2,1)S(1)} collective-permute-done((bf16[512,1536]{1,0:T(8,128)(2,1)S(1)}, bf16[512,1536]{1,0:T(8,128)(2,1)S(1)}, u32[]{:S(2)}, u32[]{:S(2)}) %collective-permute-start.2) | collective-permute-done | bytes 1572896 | tf_op jit(solution)/shard_map/ppermute | solution.py:226
  286.6 10.8 %fusion.6 = f32[1024,2048]{1,0:T(8,128)} fusion(bf16[1536,6912]{1,0:T(8,128)(2,1)} %all-gather.5.cloned.1.call-done, bf16[512,1536]{1,0:T(8,128)(2,1)S(1)} %get-tuple-element.121, bf16[512,1536]{1,0:T(8,128)(2,1)S(1)} %get-tuple-element.120), kind=kOutput, calls=%fused_computation.14 | convolution fusion | flops 6448742400 | bytes 17825792 | tf_op jit(solution)/shard_map/dot_general | solution.py:203
  297.5 17.7 %multiply_convert_fusion.1 = (bf16[1024,2048]{1,0:T(8,128)(2,1)}, bf16[1024,2048]{1,0:T(8,128)(2,1)}, bf16[1024,2048]{1,0:T(8,128)(2,1)}) fusion(f32[1024,2048]{1,0:T(8,128)} %fusion, f32[1024,2048]{1,0:T(8,128)} %fusion.6, bf16[1536,6912]{1,0:T(8,128)(2,1)} %all-gather.5.cloned.1.call-done, bf16[512,1536]{1,0:T(8,128)(2,1)} %copy-done.29, ...), kind=kOutput, calls=%fused_computation.2 | convolution fusion | flops 6482296832 | bytes 38797312 | tf_op jit(solution)/shard_map/dot_general | solution.py:203
  315.2 10.2 %fusion.4 = f32[1024,1536]{1,0:T(8,128)S(1)} fusion(bf16[1024,2048]{1,0:T(8,128)(2,1)} %get-tuple-element.114, bf16[1536,6912]{1,0:T(8,128)(2,1)} %all-gather.5.cloned.1.call-done), kind=kOutput, calls=%fused_computation.12 | convolution fusion | flops 6442450944 | bytes 16777216 | tf_op jit(solution)/shard_map/dot_general | solution.py:23
  325.4 8.8 fusion.16
  335.1 10.3 %fusion.2 = f32[1024,1536]{1,0:T(8,128)S(1)} fusion(bf16[1024,2048]{1,0:T(8,128)(2,1)} %get-tuple-element.113, bf16[1536,6912]{1,0:T(8,128)(2,1)} %all-gather.5.cloned.1.call-done), kind=kOutput, calls=%fused_computation.10 | convolution fusion | flops 6442450944 | bytes 16777216 | tf_op jit(solution)/shard_map/dot_general | solution.py:23
  347.2 24.6 %collective-permute-done.5 = bf16[512,1536]{1,0:T(8,128)(2,1)S(1)} collective-permute-done((bf16[512,1536]{1,0:T(8,128)(2,1)S(1)}, bf16[512,1536]{1,0:T(8,128)(2,1)S(1)}, u32[]{:S(2)}, u32[]{:S(2)}) %collective-permute-start.5) | collective-permute-done | bytes 1572896 | tf_op jit(solution)/shard_map/ppermute | solution.py:235
  372.8 30.2 %collective-permute-done.3 = bf16[512,1536]{1,0:T(8,128)(2,1)S(1)} collective-permute-done((bf16[512,1536]{1,0:T(8,128)(2,1)S(1)}, bf16[512,1536]{1,0:T(8,128)(2,1)S(1)}, u32[]{:S(2)}, u32[]{:S(2)}) %collective-permute-start.3) | collective-permute-done | bytes 1572896 | tf_op jit(solution)/shard_map/ppermute | solution.py:235
  406.8 33.5 %collective-permute-done.6 = bf16[512,1536]{1,0:T(8,128)(2,1)S(1)} collective-permute-done((bf16[512,1536]{1,0:T(8,128)(2,1)S(1)}, bf16[512,1536]{1,0:T(8,128)(2,1)S(1)}, u32[]{:S(2)}, u32[]{:S(2)}) %collective-permute-start.6) | collective-permute-done | bytes 1572896 | tf_op jit(solution)/shard_map/ppermute | solution.py:226
  440.5 8.0 multiply_convert_fusion.4
  448.6 37.7 %attend_backward.1 = (bf16[1024,768]{1,0:T(8,128)(2,1)S(1)}, bf16[1024,768]{1,0:T(8,128)(2,1)S(1)}, bf16[1024,768]{1,0:T(8,128)(2,1)S(1)}, f32[6,2,1024]{2,1,0:T(2,128)S(1)}, f32[6,1024,2]{2,1,0:T(8,128)}) custom-call(bf16[1024,768]{1,0:T(8,128)(2,1)} %copy-done.2, bf16[1024,768]{1,0:T(8,128)(2,1)} %copy-done.3, bf16[1024,768]{1,0:T(8,128)(2,1)} %copy-done.4, ...), custom_call_target="tpu_custom_call" | custom-call | flops 8053063680 | bytes 11010048 | tf_op jit(solution)/shard_map/attend_backward/pallas_call | solution.py:176
  543.5 16.6 %copy.145 = bf16[1536,3968]{1,0:T(8,128)(2,1)} copy(bf16[1536,3968]{0,1:T(8,128)(2,1)} %fusion.33) | data formatting | bytes 24379392
  562.0 9.7 %convolution_convert_fusion = bf16[1536,2048]{1,0:T(8,128)(2,1)S(1)} fusion(bf16[1024,2048]{1,0:T(8,128)(2,1)} %get-tuple-element.113, bf16[512,1536]{1,0:T(8,128)(2,1)S(1)} %copy-done.26, bf16[512,1536]{1,0:T(8,128)(2,1)S(1)} %copy-done.24), kind=kOutput, calls=%fused_computation.5 | convolution fusion | flops 6451888128 | bytes 13631488 | tf_op jit(solution)/shard_map/dot_general | solution.py:29
  586.5 16.4 %pad_maximum_fusion = bf16[1536,6144]{1,0:T(8,128)(2,1)} fusion(bf16[1536,2048]{1,0:T(8,128)(2,1)S(1)} %convolution_convert_fusion, bf16[1536,2048]{1,0:T(8,128)(2,1)S(1)} %convolution_convert_fusion.1, bf16[1536,2048]{1,0:T(8,128)(2,1)S(1)} %convolution_convert_fusion.2), kind=kLoop, calls=%fused_computation | loop fusion | flops 56623104 | bytes 37748736 | tf_op jit(solution)/shard_map/concatenate | solution.py:333
  603.8 15.4 %fusion.71 = f32[1024,1536]{1,0:T(8,128)S(1)} fusion(bf16[1024,3200]{1,0:T(8,128)(2,1)} %pad_dynamic-update-slice_fusion, bf16[1536,3200]{1,0:T(8,128)(2,1)} %all-gather.3.cloned.1.call-done), kind=kOutput, calls=%fused_computation.133 | convolution fusion | flops 10066329600 | bytes 22675456 | tf_op jit(solution)/shard_map/dot_general | solution.py:23
  624.1 32.4 %collective-permute-done.7 = bf16[512,1536]{1,0:T(8,128)(2,1)S(1)} collective-permute-done((bf16[512,1536]{1,0:T(8,128)(2,1)}, bf16[512,1536]{1,0:T(8,128)(2,1)S(1)}, u32[]{:S(2)}, u32[]{:S(2)}) %collective-permute-start.7) | collective-permute-done | bytes 1572896 | tf_op jit(solution)/shard_map/ppermute | solution.py:235
  659.5 42.7 %psum.7 = f32[3096]{0:T(1024)S(1)} all-reduce(f32[3096]{0:T(1024)S(1)} %pad_maximum_fusion.10), channel_id=1, replica_groups=mesh['dp'=16,'tensor'=2] {'dp','tensor'}, use_global_device_ids=true, to_apply=%region_12.13 | all-reduce | flops 3096 | bytes 24768 | tf_op jit(solution)/shard_map/psum | solution.py:368
  716.3 173.4 %reduce-scatter.5.cloned.1.call-done = bf16[96,6144]{1,0:T(8,128)(2,1)} async-done(((bf16[1536,6144]{1,0:T(8,128)(2,1)}), bf16[96,6144]{1,0:T(8,128)(2,1)}) %reduce-scatter.5.cloned.1.call-update) | async-done | bytes 1179664 | tf_op jit(solution)/shard_map/reduce_scatter | solution.py:334
  (190 shorter events, 163.6 us)
Async XLA Ops:
  7.2 88.2 %all-gather.3.cloned.1.call-start = ((), (), s32[]{:S(2)}) async-start(), calls=%async_computation.2 | async-start | bytes 10444800 | tf_op jit(solution)/shard_map/all_gather | solution.py:283
  11.7 194.5 %all-gather.5.cloned.1.call-start = ((), (), s32[]{:S(2)}) async-start(), calls=%async_computation.3 | async-start | bytes 22560768 | tf_op jit(solution)/shard_map/all_gather | solution.py:285
  14.2 695.1 %reduce-scatter.7.cloned.1.call-start = ((), (), s32[]{:S(2)}) async-start(), calls=%async_computation.5 | async-start | bytes 12951552
  14.6 84.8 %copy-start.36 = (s32[1024]{0:T(1024)S(1)}, s32[1024]{0:T(1024)}, u32[]{:S(2)}) copy-start(s32[1024]{0:T(1024)} %param.16) | copy-start | bytes 12292
  14.6 121.8 %copy-start.34 = (f32[512]{0:T(512)}, f32[512]{0:T(512)S(1)}, u32[]{:S(2)}) copy-start(f32[512]{0:T(512)S(1)} %add_rsqrt_fusion.1) | copy-start | bytes 6148
  97.3 39.2 %copy-start.32 = (f32[1536]{0:T(1024)}, f32[1536]{0:T(1024)S(1)}, u32[]{:S(2)}) copy-start(f32[1536]{0:T(1024)S(1)} %get-tuple-element.103) | copy-start | bytes 18436
  98.9 37.6 %collective-permute-start = (bf16[512,1536]{1,0:T(8,128)(2,1)}, bf16[512,1536]{1,0:T(8,128)(2,1)}, u32[]{:S(2)}, u32[]{:S(2)}) collective-permute-start(bf16[512,1536]{1,0:T(8,128)(2,1)} %fusion.25), channel_id=1, source_target_pairs={{0,1},{1,0},{2,3},{3,2},{4,5},{5,4},{6,7},{7,6},{8,9},{9,8},{10,11... | collective-permute-start | bytes 4718600 | tf_op jit(solution)/shard_map/ppermute | solution.py:226
  102.3 109.6 %collective-permute-start.4 = (bf16[512,1536]{1,0:T(8,128)(2,1)}, bf16[512,1536]{1,0:T(8,128)(2,1)}, u32[]{:S(2)}, u32[]{:S(2)}) collective-permute-start(bf16[512,1536]{1,0:T(8,128)(2,1)} %broadcast_select_fusion), channel_id=1, source_target_pairs={{0,1},{1,0},{2,3},{3,2},{4,5},{5,4},{6,7},{7,6},{8,9},{9,8},{10,11... | collective-permute-start | bytes 4718600 | tf_op jit(solution)/shard_map/ppermute | solution.py:226
  164.1 32.8 %copy-start.4 = (bf16[1024,768]{1,0:T(8,128)(2,1)}, bf16[1024,768]{1,0:T(8,128)(2,1)S(1)}, u32[]{:S(2)}) copy-start(bf16[1024,768]{1,0:T(8,128)(2,1)S(1)} %fusion.52.v_ref) | copy-start | bytes 4718596
  211.2 36.6 %collective-permute-start.1 = (bf16[512,1536]{1,0:T(8,128)(2,1)S(1)}, bf16[512,1536]{1,0:T(8,128)(2,1)S(1)}, u32[]{:S(2)}, u32[]{:S(2)}) collective-permute-start(bf16[512,1536]{1,0:T(8,128)(2,1)S(1)} %dynamic-slice_convert_fusion.3), channel_id=1, source_target_pairs={{0,1},{1,0},{2,3},{3,2},{4,5},{5,4},{6,7},{7,6},{8,9},{9,8},{10,11... | collective-permute-start | bytes 4718600 | tf_op jit(solution)/shard_map/ppermute | solution.py:235
  214.1 35.4 %copy-start.23 = (bf16[512,1536]{1,0:T(8,128)(2,1)}, bf16[512,1536]{1,0:T(8,128)(2,1)S(1)}, u32[]{:S(2)}) copy-start(bf16[512,1536]{1,0:T(8,128)(2,1)S(1)} %get-tuple-element.118) | copy-start | bytes 4718596
  214.1 35.4 %copy-start.25 = (bf16[512,1536]{1,0:T(8,128)(2,1)}, bf16[512,1536]{1,0:T(8,128)(2,1)S(1)}, u32[]{:S(2)}) copy-start(bf16[512,1536]{1,0:T(8,128)(2,1)S(1)} %get-tuple-element.119) | copy-start | bytes 4718596
  248.9 35.8 %collective-permute-start.2 = (bf16[512,1536]{1,0:T(8,128)(2,1)S(1)}, bf16[512,1536]{1,0:T(8,128)(2,1)S(1)}, u32[]{:S(2)}, u32[]{:S(2)}) collective-permute-start(bf16[512,1536]{1,0:T(8,128)(2,1)S(1)} %multiply_convert_fusion.5), channel_id=1, source_target_pairs={{0,1},{1,0},{2,3},{3,2},{4,5},{5,4},{6,7},{7,6},{8,9},{9,8},{10,11... | collective-permute-start | bytes 4718600 | tf_op jit(solution)/shard_map/ppermute | solution.py:226
  285.4 12.1 %copy-start.27 = (bf16[512,1536]{1,0:T(8,128)(2,1)}, bf16[512,1536]{1,0:T(8,128)(2,1)S(1)}, u32[]{:S(2)}) copy-start(bf16[512,1536]{1,0:T(8,128)(2,1)S(1)} %get-tuple-element.120) | copy-start | bytes 4718596
  334.5 37.3 %collective-permute-start.5 = (bf16[512,1536]{1,0:T(8,128)(2,1)S(1)}, bf16[512,1536]{1,0:T(8,128)(2,1)S(1)}, u32[]{:S(2)}, u32[]{:S(2)}) collective-permute-start(bf16[512,1536]{1,0:T(8,128)(2,1)S(1)} %dynamic-slice_convert_fusion.1), channel_id=1, source_target_pairs={{0,1},{1,0},{2,3},{3,2},{4,5},{5,4},{6,7},{7,6},{8,9},{9,8},{10,11... | collective-permute-start | bytes 4718600 | tf_op jit(solution)/shard_map/ppermute | solution.py:235
  345.6 57.5 %copy-start.8 = (bf16[512,1536]{1,0:T(8,128)(2,1)S(1)}, bf16[512,1536]{1,0:T(8,128)(2,1)}, u32[]{:S(2)}) copy-start(bf16[512,1536]{1,0:T(8,128)(2,1)} %param.29) | copy-start | bytes 4718596
  345.6 57.5 %collective-permute-start.3 = (bf16[512,1536]{1,0:T(8,128)(2,1)S(1)}, bf16[512,1536]{1,0:T(8,128)(2,1)S(1)}, u32[]{:S(2)}, u32[]{:S(2)}) collective-permute-start(bf16[512,1536]{1,0:T(8,128)(2,1)S(1)} %dynamic-slice_convert_fusion.2), channel_id=1, source_target_pairs={{0,1},{1,0},{2,3},{3,2},{4,5},{5,4},{6,7},{7,6},{8,9},{9,8},{10,11... | collective-permute-start | bytes 4718600 | tf_op jit(solution)/shard_map/ppermute | solution.py:235
  406.3 34.2 %copy-start.11 = (f32[1024,768]{1,0:T(8,128)S(1)}, f32[1024,768]{1,0:T(8,128)}, u32[]{:S(2)}) copy-start(f32[1024,768]{1,0:T(8,128)} %get-tuple-element.137) | copy-start | bytes 9437188
  406.3 34.0 %collective-permute-start.6 = (bf16[512,1536]{1,0:T(8,128)(2,1)S(1)}, bf16[512,1536]{1,0:T(8,128)(2,1)S(1)}, u32[]{:S(2)}, u32[]{:S(2)}) collective-permute-start(bf16[512,1536]{1,0:T(8,128)(2,1)S(1)} %get-tuple-element.108), channel_id=1, source_target_pairs={{0,1},{1,0},{2,3},{3,2},{4,5},{5,4},{6,7},{7,6},{8,9},{9,8},{10,11... | collective-permute-start | bytes 4718600 | tf_op jit(solution)/shard_map/ppermute | solution.py:226
  560.1 329.6 %reduce-scatter.5.cloned.1.call-start = ((), (), s32[]{:S(2)}) async-start(), calls=%async_computation.4 | async-start | bytes 20054016 | tf_op jit(solution)/shard_map/reduce_scatter | solution.py:334
  621.9 34.7 %copy-start.6 = (bf16[512,1536]{1,0:T(8,128)(2,1)S(1)}, bf16[512,1536]{1,0:T(8,128)(2,1)}, u32[]{:S(2)}) copy-start(bf16[512,1536]{1,0:T(8,128)(2,1)} %param.15) | copy-start | bytes 4718596
  621.9 34.7 %copy-start.33 = (f32[1536]{0:T(1024)S(1)}, f32[1536]{0:T(1024)}, u32[]{:S(2)}) copy-start(f32[1536]{0:T(1024)} %copy-done.32) | copy-start | bytes 18436
  621.9 34.7 %copy-start.35 = (f32[512]{0:T(512)S(1)}, f32[512]{0:T(512)}, u32[]{:S(2)}) copy-start(f32[512]{0:T(512)} %copy-done.34) | copy-start | bytes 6148
  623.2 33.3 %collective-permute-start.7 = (bf16[512,1536]{1,0:T(8,128)(2,1)}, bf16[512,1536]{1,0:T(8,128)(2,1)S(1)}, u32[]{:S(2)}, u32[]{:S(2)}) collective-permute-start(bf16[512,1536]{1,0:T(8,128)(2,1)} %dynamic-slice_convert_fusion), channel_id=1, source_target_pairs={{0,1},{1,0},{2,3},{3,2},{4,5},{5,4},{6,7},{7,6},{8,9},{9,8},{10,11... | collective-permute-start | bytes 4718600 | tf_op jit(solution)/shard_map/ppermute | solution.py:235
  (29 other events, 145.7 us)
Sparse Core Ops, SparseCore 0:
  11.8 83.5 all-gather.2
  97.0 109.1 all-gather.4
  560.2 132.2 reduce-scatter.6
  696.4 193.2 reduce-scatter.4
